TPU v7x, 32 devices: a whole 2x2x4 slice. The times are simulated.
32 devices in a mesh: unit: 4 (over z), zero: 2 (over x), tp: 4 (over y, core).
Axes of the slice: x: 2, y: 2, z: 4, core: 2. Of those that a mesh axis runs over, the one named last changes fastest.
Arguments:
- weight_query: bfloat16 [16384, 4096], P(('unit', 'zero'), 'tp'), parts along dimension 0, may hold values from -0.125 to 0.125
- low_query: bfloat16 [16384, 32], P(('unit', 'zero')), parts along dimension 0, may hold values from -0.09375 to 0.09375
- high_query: bfloat16 [128, 4096], P('unit', 'tp'), parts along dimension 0, may hold values from -1 to 1
- weight_key: bfloat16 [16384, 1024], P(('unit', 'zero'), 'tp'), parts along dimension 0, may hold values from -0.125 to 0.125
- low_key: bfloat16 [16384, 32], P(('unit', 'zero')), parts along dimension 0, may hold values from -0.09375 to 0.09375
- high_key: bfloat16 [128, 1024], P('unit', 'tp'), parts along dimension 0, may hold values from -1 to 1
- weight_value: bfloat16 [16384, 1024], P(('unit', 'zero'), 'tp'), parts along dimension 0, may hold values from -0.125 to 0.125
- low_value: bfloat16 [16384, 32], P(('unit', 'zero')), parts along dimension 0, may hold values from -0.09375 to 0.09375
- high_value: bfloat16 [128, 1024], P('unit', 'tp'), parts along dimension 0, may hold values from -1 to 1
- norm_train: float32 [16384], P(('unit', 'zero', 'tp')), parts along dimension 0, may hold values from 0.25 to 1.75
- norm_step: float32 [16384], P(('unit', 'zero', 'tp')), parts along dimension 0, may hold values from -0.3 to 0.3
Outputs:
- serve_query: bfloat16 [16384, 4096], P('unit', 'tp'), parts along dimension 0
- serve_key: bfloat16 [16384, 1024], P('unit', 'tp'), parts along dimension 0
- serve_value: bfloat16 [16384, 1024], P('unit', 'tp'), parts along dimension 0
- column_query: float32 [16384], P(('unit', 'tp')), parts along dimension 0
- column_key: float32 [4096], P(('unit', 'tp')), parts along dimension 0
- column_value: float32 [4096], P(('unit', 'tp')), parts along dimension 0
- serve_norm: bfloat16 [16384], P('unit'), parts along dimension 0
There are 4 independent parts, one for each index of `unit`. A program takes and returns all parts, laid end to end along the dimension named above; each array names one. Nothing has to cross between parts.
All inputs are finite; a program needn't handle non-finite values.
Results may differ from a plain program's by a relative error of at most 0.001.
Values may be sent and summed in bfloat16 or wider, within the bound.
A program may use at most 64 MiB of HBM per device.

v0:
```python
import functools

import jax
import jax.numpy as jnp
from jax import lax
from jax.experimental import pallas as pl
from jax.experimental.pallas import tpu as pltpu
from jax.sharding import PartitionSpec as P

mix_rate = 2.0


def finish_kernel(n, rows, tile, extra, *refs):
    own_ref, others, low_ref, high_ref = refs[0], refs[1:n], refs[n], refs[n + 1]
    out_ref, col_ref, fresh, total = refs[n + 2 + extra :]
    me = lax.axis_index("zero")
    total[...] = jnp.zeros_like(total)
    width = out_ref.shape[1]
    for slot, piece in enumerate((own_ref,) + tuple(others)):
        giver = lax.rem(me + n - slot, n)

        @pl.loop(0, rows // tile)
        def _(t):
            at = pl.multiple_of(t * tile, tile)
            merged = piece[pl.ds(at, tile), :].astype(jnp.float32) + mix_rate * lax.dot_general(
                low_ref[slot, pl.ds(at, tile), :],
                high_ref[...],
                (((1,), (0,)), ((), ())),
                preferred_element_type=jnp.float32,
            )
            fresh[pl.ds(pl.multiple_of(slot * rows + at, tile), tile), :] = merged
            total[giver] += jnp.sum((merged * merged).reshape(tile // 8, 8, width), axis=0)

    column = jnp.sqrt(jnp.sum(jnp.sum(total[...], axis=0), axis=0, keepdims=True))
    col_ref[...] = column
    inverse = 1.0 / column
    for slot in range(n):
        owner = lax.rem(me + n - slot, n)

        @pl.loop(0, rows // tile)
        def _(t):
            at = pl.multiple_of(t * tile, tile)
            out_ref[pl.ds(pl.multiple_of(owner * rows + at, tile), tile), :] = (
                fresh[pl.ds(pl.multiple_of(slot * rows + at, tile), tile), :] * inverse
            ).astype(out_ref.dtype)


def finish(n, weight, others, low, high, after):
    rows, width = weight.shape
    rank = high.shape[0]
    tile = min(rows, 256)
    args = [weight, *others, low, high]
    specs = (
        [pl.BlockSpec((rows, width), lambda i: (0, 0))]
        + [pl.BlockSpec((rows, width), lambda i: (0, 0))] * (n - 1)
        + [
            pl.BlockSpec((n, rows, rank), lambda i: (0, 0, 0)),
            pl.BlockSpec((rank, width), lambda i: (0, 0)),
        ]
    )
    if after is not None:
        args.append(after)
    extra = len(args) - len(specs)
    specs += [pl.BlockSpec(memory_space=pl.ANY)] * extra
    elements = n * rows * width
    return pl.pallas_call(
        functools.partial(finish_kernel, n, rows, tile, extra),
        grid=(1,),
        out_shape=(
            jax.ShapeDtypeStruct((n * rows, width), jnp.bfloat16),
            jax.ShapeDtypeStruct((1, width), jnp.float32),
        ),
        in_specs=specs,
        out_specs=(
            pl.BlockSpec((n * rows, width), lambda i: (0, 0)),
            pl.BlockSpec((1, width), lambda i: (0, 0)),
        ),
        scratch_shapes=[
            pltpu.VMEM((n * rows, width), jnp.float32),
            pltpu.VMEM((n, 8, width), jnp.float32),
        ],
        cost_estimate=pl.CostEstimate(
            flops=2 * elements * rank, bytes_accessed=8 * elements, transcendentals=0
        ),
    )(*args)


def merge(piece, low, high):
    return piece.astype(jnp.float32) + mix_rate * jnp.dot(
        low, high, preferred_element_type=jnp.float32
    )


def groups(full):
    wide = min(256, full)
    return [pl.ds(s, wide) for s in range(0, full, wide)]


def sums_kernel(weight_ref, low_ref, high_ref, sum_ref):
    @pl.when(pl.program_id(0) == 0)
    def _():
        sum_ref[...] = jnp.zeros_like(sum_ref)

    for at in groups(sum_ref.shape[1]):
        merged = merge(weight_ref[:, at], low_ref[...], high_ref[:, at])
        sum_ref[:, at] += jnp.sum(merged * merged, axis=0, keepdims=True)


def serve_kernel(weight_ref, low_ref, high_ref, column_ref, out_ref):
    for at in groups(out_ref.shape[1]):
        merged = merge(weight_ref[:, at], low_ref[...], high_ref[:, at])
        out_ref[:, at] = (merged * (1.0 / column_ref[:, at])).astype(out_ref.dtype)


def own_rows(kernel, weight, low, high, column, start, size):
    full, rank = weight.shape[1], high.shape[0]
    tile = min(size, 256)
    first = start // tile
    args = [weight, low, high]
    specs = [
        pl.BlockSpec((tile, full), lambda i: (first + i, 0)),
        pl.BlockSpec((tile, rank), lambda i: (first + i, 0)),
        pl.BlockSpec((rank, full), lambda i: (0, 0)),
    ]
    line = pl.BlockSpec((1, full), lambda i: (0, 0))
    if column is None:
        out_shape, out_spec = jax.ShapeDtypeStruct((1, full), jnp.float32), line
    else:
        args.append(column)
        specs.append(line)
        out_shape = jax.ShapeDtypeStruct((size, full), jnp.bfloat16)
        out_spec = pl.BlockSpec((tile, full), lambda i: (i, 0))
    return pl.pallas_call(
        kernel,
        grid=(size // tile,),
        out_shape=out_shape,
        in_specs=specs,
        out_specs=out_spec,
        cost_estimate=pl.CostEstimate(
            flops=2 * size * full * rank, bytes_accessed=4 * size * full, transcendentals=0
        ),
    )(*args)


def on_device(
    n,
    parts,
    weight_query,
    low_query,
    high_query,
    weight_key,
    low_key,
    high_key,
    weight_value,
    low_value,
    high_value,
    norm_train,
    norm_step,
):
    rows = weight_query.shape[0]
    rank = high_query.shape[0]
    me, tp = lax.axis_index("zero"), lax.axis_index("tp")

    def shifted(array):
        return [
            lax.ppermute(array, "zero", [(i, (i + k) % n) for i in range(n)])
            for k in range(1, n)
        ]

    def in_order(mine, others, axis):
        size = mine.shape[axis]
        shape = list(mine.shape)
        shape[axis] *= n
        whole = jnp.zeros(shape, mine.dtype)
        for slot, piece in enumerate([mine] + list(others)):
            at = [0] * len(shape)
            at[axis] = (me + n - slot) % n * size
            whole = lax.dynamic_update_slice(whole, piece, at)
        return whole

    value_parts = shifted(weight_value)

    piece = rows // parts
    lows = [
        lax.dynamic_slice(low, (tp * piece, 0), (piece, rank)).T
        for low in (low_key, low_value)
    ]
    norm = (norm_train + norm_step).astype(jnp.bfloat16)
    packed = jnp.concatenate(lows + [norm.reshape(-1, piece)], axis=0)
    shape = packed.shape
    if packed.size % 128 == 0:
        packed = packed.reshape(-1, 128)
    sent = shifted(packed)
    total = own_rows(sums_kernel, weight_query, low_query, high_query, None, 0, rows)
    totals = in_order(total, shifted(total), 0)
    column_query = jnp.sqrt(jnp.sum(totals, axis=0, keepdims=True))
    key_parts = shifted(weight_key)

    sizes = [rows // 2, rows // 4, rows // 8, rows // 16]
    sizes.append(rows - sum(sizes))
    mine, theirs, start = [], [], 0
    for size in sizes:
        chunk = own_rows(serve_kernel, weight_query, low_query, high_query, column_query, start, size)
        mine.append((start, chunk))
        theirs.append((start, shifted(chunk)))
        start += size

    packs = jnp.stack([a.reshape(shape) for a in [packed] + sent])
    packs = lax.all_gather(packs, "tp", axis=2, tiled=True)
    low_all = jnp.swapaxes(packs[:, : 2 * rank], 1, 2)
    gain = packs[:, 2 * rank :].reshape(n, -1, parts, piece)
    gain = jnp.swapaxes(gain, 1, 2).reshape(n, -1)
    serve_norm = in_order(gain[:1], [gain[k : k + 1] for k in range(1, n)], 0).reshape(-1)
    serve_value, column_value = finish(
        n, weight_value, value_parts, low_all[:, :, rank:], high_value, None
    )
    serve_key, column_key = finish(
        n, weight_key, key_parts, low_all[:, :, :rank], high_key, column_value
    )
    serve_query = jnp.zeros((n * rows, weight_query.shape[1]), jnp.bfloat16)
    for start, chunk in mine:
        serve_query = lax.dynamic_update_slice(serve_query, chunk, (me * rows + start, 0))
    for start, arrived in theirs:
        for k, chunk in enumerate(arrived):
            owner = (me + n - 1 - k) % n
            serve_query = lax.dynamic_update_slice(serve_query, chunk, (owner * rows + start, 0))
    return (
        serve_query,
        serve_key,
        serve_value,
        column_query.reshape(-1),
        column_key.reshape(-1),
        column_value.reshape(-1),
        serve_norm,
    )


def solution(mesh):
    placed = (
        P(("unit", "zero"), "tp"),
        P(("unit", "zero"), None),
        P("unit", "tp"),
        P(("unit", "zero"), "tp"),
        P(("unit", "zero"), None),
        P("unit", "tp"),
        P(("unit", "zero"), "tp"),
        P(("unit", "zero"), None),
        P("unit", "tp"),
        P(("unit", "zero", "tp")),
        P(("unit", "zero", "tp")),
    )

    def body(*args):
        return on_device(mesh.shape["zero"], mesh.shape["tp"], *args)

    return jax.shard_map(
        body,
        mesh=mesh,
        in_specs=placed,
        out_specs=(
            P("unit", "tp"),
            P("unit", "tp"),
            P("unit", "tp"),
            P(("unit", "tp")),
            P(("unit", "tp")),
            P(("unit", "tp")),
            P("unit"),
        ),
        check_vma=False,
    )
```

profile of v0, /device:TPU:0, one launch (start us, length us, event | category | flops | bytes accessed | tf_op | source)
XLA Modules:
  0.0 153.6 jit_solution(4678748190741722549)
XLA Ops:
  0.6 1.9 %copy.27.low_ref = bf16[2048,32]{1,0:T(8,128)(2,1)} copy(bf16[2048,32]{0,1:T(8,128)(2,1)} %param.12) | data formatting | bytes 262144 | tf_op args[1]
  2.5 6.7 %shard_map.162 = f32[1,1024]{1,0:T(1,128)} custom-call(bf16[2048,1024]{1,0:T(8,128)(2,1)} %weight_ref.11, bf16[2048,32]{1,0:T(8,128)(2,1)} %copy.27.low_ref, bf16[32,1024]{1,0:T(8,128)(2,1)} %high_ref.11), custom_call_target="tpu_custom_call" | custom-call | flops 134217728 | bytes 8388608 | tf_op jit(solution)/shard_map/pallas_call | solution.py:133
  9.2 3.0 %collective-permute-start = (f32[1,1024]{1,0:T(1,128)}, f32[1,1024]{1,0:T(1,128)S(1)}, u32[]{:S(2)}, u32[]{:S(2)}) collective-permute-start(f32[1,1024]{1,0:T(1,128)} %shard_map.162), channel_id=1, source_target_pairs={{0,4},{4,0},{1,5},{5,1},{2,6},{6,2},{3,7},{7,3},{8,12},{12,8},{9,1... | collective-permute-start | bytes 12296 | tf_op jit(solution)/shard_map/ppermute | solution.py:166
  12.2 0.8 constant_dynamic-slice_fusion
  13.0 0.1 copy.37
  13.1 0.1 copy.38
  13.2 0.7 add_convert_fusion
  13.9 0.1 reshape.46
  14.1 0.1 pad_maximum_fusion.1
  14.2 0.1 copy.35
  14.3 0.1 reshape.42
  14.4 0.1 collective-permute-start.7
  14.5 2.0 %collective-permute-start.8 = (bf16[2048,256]{1,0:T(8,128)(2,1)}, bf16[2048,256]{1,0:T(8,128)(2,1)S(1)}, u32[]{:S(2)}, u32[]{:S(2)}) collective-permute-start(bf16[2048,256]{1,0:T(8,128)(2,1)} %refs_0_.2), channel_id=1, source_target_pairs={{0,4},{4,0},{1,5},{5,1},{2,6},{6,2},{3,7},{7,3},{8,12},{12,8},{9,1... | collective-permute-start | bytes 3145736 | tf_op jit(solution)/shard_map/ppermute | solution.py:166
  16.5 0.1 collective-permute-start.6
  16.6 0.1 fusion.1
  16.8 0.7 dynamic_update_slice.42
  17.6 0.0 collective-permute-done
  17.6 0.1 dynamic_update_slice.43
  17.7 0.6 sqrt.5
  18.3 4.3 %shard_map.163 = bf16[1024,1024]{1,0:T(8,128)(2,1)} custom-call(bf16[2048,1024]{1,0:T(8,128)(2,1)} %weight_ref.11, bf16[2048,32]{1,0:T(8,128)(2,1)} %copy.27.low_ref, bf16[32,1024]{1,0:T(8,128)(2,1)} %high_ref.11, f32[1,1024]{1,0:T(1,128)} %bitcast.15), custom_call_target="tpu_custom_call" | custom-call | flops 67108864 | bytes 4194304 | tf_op jit(solution)/shard_map/pallas_call | solution.py:133
  22.6 2.6 %shard_map.164 = bf16[512,1024]{1,0:T(8,128)(2,1)} custom-call(bf16[2048,1024]{1,0:T(8,128)(2,1)} %weight_ref.11, bf16[2048,32]{1,0:T(8,128)(2,1)} %copy.27.low_ref, bf16[32,1024]{1,0:T(8,128)(2,1)} %high_ref.11, f32[1,1024]{1,0:T(1,128)} %bitcast.16), custom_call_target="tpu_custom_call" | custom-call | flops 33554432 | bytes 2097152 | tf_op jit(solution)/shard_map/pallas_call | solution.py:133
  25.2 2.0 %collective-permute-start.1 = (bf16[1024,1024]{1,0:T(8,128)(2,1)}, bf16[1024,1024]{1,0:T(8,128)(2,1)}, u32[]{:S(2)}, u32[]{:S(2)}) collective-permute-start(bf16[1024,1024]{1,0:T(8,128)(2,1)} %shard_map.163), channel_id=1, source_target_pairs={{0,4},{4,0},{1,5},{5,1},{2,6},{6,2},{3,7},{7,3},{8,12},{12,8},{9,1... | collective-permute-start | bytes 6291464 | tf_op jit(solution)/shard_map/ppermute | solution.py:166
  27.2 0.1 collective-permute-start.2
  27.2 4.5 %broadcast_in_dim.10 = bf16[4096,1024]{1,0:T(8,128)(2,1)} broadcast(bf16[]{:T(256)} %constant.57.clone.1), dimensions={} | broadcast | bytes 8388610 | tf_op jit(solution)/shard_map/broadcast_in_dim | solution.py:220
  31.7 0.0 copy-done
  31.7 1.5 constant_dynamic-update-slice_fusion.9
  33.2 2.0 %shard_map.166 = bf16[128,1024]{1,0:T(8,128)(2,1)} custom-call(bf16[2048,1024]{1,0:T(8,128)(2,1)} %weight_ref.11, bf16[2048,32]{1,0:T(8,128)(2,1)} %copy.27.low_ref, bf16[32,1024]{1,0:T(8,128)(2,1)} %high_ref.11, f32[1,1024]{1,0:T(1,128)} %bitcast.17), custom_call_target="tpu_custom_call" | custom-call | flops 8388608 | bytes 524288 | tf_op jit(solution)/shard_map/pallas_call | solution.py:133
  35.2 1.9 %shard_map.167 = bf16[128,1024]{1,0:T(8,128)(2,1)} custom-call(bf16[2048,1024]{1,0:T(8,128)(2,1)} %weight_ref.11, bf16[2048,32]{1,0:T(8,128)(2,1)} %copy.27.low_ref, bf16[32,1024]{1,0:T(8,128)(2,1)} %high_ref.11, f32[1,1024]{1,0:T(1,128)} %bitcast.18), custom_call_target="tpu_custom_call" | custom-call | flops 8388608 | bytes 524288 | tf_op jit(solution)/shard_map/pallas_call | solution.py:133
  37.1 2.2 %shard_map.165 = bf16[256,1024]{1,0:T(8,128)(2,1)} custom-call(bf16[2048,1024]{1,0:T(8,128)(2,1)} %weight_ref.11, bf16[2048,32]{1,0:T(8,128)(2,1)} %copy.27.low_ref, bf16[32,1024]{1,0:T(8,128)(2,1)} %high_ref.11, f32[1,1024]{1,0:T(1,128)} %bitcast.19), custom_call_target="tpu_custom_call" | custom-call | flops 16777216 | bytes 1048576 | tf_op jit(solution)/shard_map/pallas_call | solution.py:133
  39.3 0.0 copy-done.1
  39.3 1.0 constant_dynamic-update-slice_fusion.8
  40.3 1.9 %constant_dynamic-update-slice_fusion.7 = bf16[4096,1024]{1,0:T(8,128)(2,1)} fusion(bf16[4096,1024]{1,0:T(8,128)(2,1)} %constant_dynamic-update-slice_fusion.8, bf16[256,1024]{1,0:T(8,128)(2,1)} %shard_map.165, s32[]{:T(128)S(6)} %select_n.73), kind=kLoop, calls=%fused_computation.14 | loop fusion | bytes 1048580 | tf_op jit(solution)/shard_map/dynamic_update_slice | solution.py:222
  42.2 0.0 copy-done.4
  42.2 0.7 constant_dynamic-update-slice_fusion.6
  42.9 0.7 constant_dynamic-update-slice_fusion.5
  43.7 0.0 collective-permute-done.7
  43.7 2.0 %collective-permute-start.3 = (bf16[256,1024]{1,0:T(8,128)(2,1)}, bf16[256,1024]{1,0:T(8,128)(2,1)S(1)}, u32[]{:S(2)}, u32[]{:S(2)}) collective-permute-start(bf16[256,1024]{1,0:T(8,128)(2,1)} %shard_map.165), channel_id=1, source_target_pairs={{0,4},{4,0},{1,5},{5,1},{2,6},{6,2},{3,7},{7,3},{8,12},{12,8},{9,1... | collective-permute-start | bytes 1572872 | tf_op jit(solution)/shard_map/ppermute | solution.py:166
  45.6 0.1 stack_reshape.3
  45.7 0.1 copy.36
  45.8 0.1 pad_maximum_fusion
  45.9 10.0 %all_gather.3 = bf16[2,65,2048]{1,2,0:T(8,128)(2,1)S(1)} all-gather(bf16[2,65,512]{1,2,0:T(8,128)(2,1)S(1)} %pad_maximum_fusion), channel_id=1, replica_groups=mesh['unit'=4,'zero'=2,'tp'=4] {'tp'}, dimensions={2}, use_global_device_ids=true | all-gather | bytes 665600 | tf_op jit(solution)/shard_map/all_gather | solution.py:209
  55.9 0.1 slice_bitcast_fusion
  56.0 1.7 %fusion = (bf16[2,2048,32]{2,1,0:T(8,128)(2,1)}, bf16[2,2048,32]{2,1,0:T(8,128)(2,1)}) fusion(bf16[2,2048,64]{2,1,0:T(8,128)(2,1)S(1)} %slice_bitcast_fusion), kind=kLoop, calls=%fused_computation.18 | loop fusion | bytes 1048576 | tf_op jit(solution)/shard_map/slice | solution.py:215
  57.7 0.7 slice_reduce_fusion
  58.5 0.1 dynamic_update_slice.54
  58.5 0.1 dynamic_update_slice.55
  58.6 0.6 copy.39
  59.2 0.0 collective-permute-done.8.refs_1_
  59.2 0.5 collective-permute-start.4
  59.7 0.5 copy-done.2
  60.3 6.4 %shard_map.168 = (bf16[4096,256]{1,0:T(8,128)(2,1)}, f32[1,256]{1,0:T(1,128)}) custom-call(bf16[2048,256]{1,0:T(8,128)(2,1)} %refs_0_.2, bf16[2048,256]{1,0:T(8,128)(2,1)} %copy-done.2, bf16[2,2048,32]{2,1,0:T(8,128)(2,1)} %get-tuple-element.17.refs_2_, bf16[32,256]{1,0:T(8,128)(2,1)} %refs_3_.2), custom_call_target="tpu_custom_call" | custom-call | flops 67108864 | bytes 8388608 | tf_op jit(solution)/shard_map/pallas_call | solution.py:66
  66.7 0.0 collective-permute-done.6.refs_1_
  66.7 1.0 collective-permute-start.5
  67.6 6.4 %shard_map.169 = (bf16[4096,256]{1,0:T(8,128)(2,1)}, f32[1,256]{1,0:T(1,128)}) custom-call(bf16[2048,256]{1,0:T(8,128)(2,1)} %refs_0_.3, bf16[2048,256]{1,0:T(8,128)(2,1)} %collective-permute-done.6.refs_1_, bf16[2,2048,32]{2,1,0:T(8,128)(2,1)} %get-tuple-element.18.refs_2_, bf16[32,256]{1,0:T(8,128)(2,1)} %refs_3_.3, f32[1,256]{1,0:T(1,128)} %get-tuple-element.11.refs_4_), custom_call_target="tpu_custom_call" | custom-call | flops 67108864 | bytes 8388608 | tf_op jit(solution)/shard_map/pallas_call | solution.py:66
  74.1 35.4 %collective-permute-done.1 = bf16[1024,1024]{1,0:T(8,128)(2,1)} collective-permute-done((bf16[1024,1024]{1,0:T(8,128)(2,1)}, bf16[1024,1024]{1,0:T(8,128)(2,1)}, u32[]{:S(2)}, u32[]{:S(2)}) %collective-permute-start.1) | collective-permute-done | bytes 2097184 | tf_op jit(solution)/shard_map/ppermute | solution.py:166
  109.5 3.1 %constant_dynamic-update-slice_fusion.4 = bf16[4096,1024]{1,0:T(8,128)(2,1)} fusion(bf16[4096,1024]{1,0:T(8,128)(2,1)} %constant_dynamic-update-slice_fusion.5, bf16[1024,1024]{1,0:T(8,128)(2,1)} %collective-permute-done.1, s32[]{:T(128)S(6)} %select_n.76), kind=kLoop, calls=%fused_computation.11 | loop fusion | bytes 4194308 | tf_op jit(solution)/shard_map/dynamic_update_slice | solution.py:226
  112.6 19.4 %collective-permute-done.2 = bf16[512,1024]{1,0:T(8,128)(2,1)} collective-permute-done((bf16[512,1024]{1,0:T(8,128)(2,1)}, bf16[512,1024]{1,0:T(8,128)(2,1)}, u32[]{:S(2)}, u32[]{:S(2)}) %collective-permute-start.2) | collective-permute-done | bytes 1048608 | tf_op jit(solution)/shard_map/ppermute | solution.py:166
  131.9 2.3 %constant_dynamic-update-slice_fusion.3 = bf16[4096,1024]{1,0:T(8,128)(2,1)} fusion(bf16[4096,1024]{1,0:T(8,128)(2,1)} %constant_dynamic-update-slice_fusion.4, bf16[512,1024]{1,0:T(8,128)(2,1)} %collective-permute-done.2, s32[]{:T(128)S(6)} %select_n.77), kind=kLoop, calls=%fused_computation.10 | loop fusion | bytes 2097156 | tf_op jit(solution)/shard_map/dynamic_update_slice | solution.py:226
  134.2 8.9 %collective-permute-done.3 = bf16[256,1024]{1,0:T(8,128)(2,1)S(1)} collective-permute-done((bf16[256,1024]{1,0:T(8,128)(2,1)}, bf16[256,1024]{1,0:T(8,128)(2,1)S(1)}, u32[]{:S(2)}, u32[]{:S(2)}) %collective-permute-start.3) | collective-permute-done | bytes 524320 | tf_op jit(solution)/shard_map/ppermute | solution.py:166
  143.1 0.8 constant_dynamic-update-slice_fusion.2
  143.9 4.8 %collective-permute-done.4 = bf16[128,1024]{1,0:T(8,128)(2,1)S(1)} collective-permute-done((bf16[128,1024]{1,0:T(8,128)(2,1)S(1)}, bf16[128,1024]{1,0:T(8,128)(2,1)S(1)}, u32[]{:S(2)}, u32[]{:S(2)}) %collective-permute-start.4) | collective-permute-done | bytes 262176 | tf_op jit(solution)/shard_map/ppermute | solution.py:166
  148.7 0.7 constant_dynamic-update-slice_fusion.1
  149.4 3.5 %collective-permute-done.5 = bf16[128,1024]{1,0:T(8,128)(2,1)S(1)} collective-permute-done((bf16[128,1024]{1,0:T(8,128)(2,1)S(1)}, bf16[128,1024]{1,0:T(8,128)(2,1)S(1)}, u32[]{:S(2)}, u32[]{:S(2)}) %collective-permute-start.5) | collective-permute-done | bytes 262176 | tf_op jit(solution)/shard_map/ppermute | solution.py:166
  152.9 0.7 constant_dynamic-update-slice_fusion
  (11 shorter events, 0.1 us)
Async XLA Ops:
  9.2 8.4 %collective-permute-start = (f32[1,1024]{1,0:T(1,128)}, f32[1,1024]{1,0:T(1,128)S(1)}, u32[]{:S(2)}, u32[]{:S(2)}) collective-permute-start(f32[1,1024]{1,0:T(1,128)} %shard_map.162), channel_id=1, source_target_pairs={{0,4},{4,0},{1,5},{5,1},{2,6},{6,2},{3,7},{7,3},{8,12},{12,8},{9,1... | collective-permute-start | bytes 12296 | tf_op jit(solution)/shard_map/ppermute | solution.py:166
  14.4 29.2 %collective-permute-start.7 = (bf16[260,128]{1,0:T(8,128)(2,1)S(1)}, bf16[260,128]{1,0:T(8,128)(2,1)S(1)}, u32[]{:S(2)}, u32[]{:S(2)}) collective-permute-start(bf16[260,128]{1,0:T(8,128)(2,1)S(1)} %reshape.42), channel_id=1, source_target_pairs={{0,4},{4,0},{1,5},{5,1},{2,6},{6,2},{3,7},{7,3},{8,12},{12,8},{9,1... | collective-permute-start | bytes 199688 | tf_op jit(solution)/shard_map/ppermute | solution.py:166
  14.5 44.7 %collective-permute-start.8 = (bf16[2048,256]{1,0:T(8,128)(2,1)}, bf16[2048,256]{1,0:T(8,128)(2,1)S(1)}, u32[]{:S(2)}, u32[]{:S(2)}) collective-permute-start(bf16[2048,256]{1,0:T(8,128)(2,1)} %refs_0_.2), channel_id=1, source_target_pairs={{0,4},{4,0},{1,5},{5,1},{2,6},{6,2},{3,7},{7,3},{8,12},{12,8},{9,1... | collective-permute-start | bytes 3145736 | tf_op jit(solution)/shard_map/ppermute | solution.py:166
  16.5 50.2 %collective-permute-start.6 = (bf16[2048,256]{1,0:T(8,128)(2,1)}, bf16[2048,256]{1,0:T(8,128)(2,1)}, u32[]{:S(2)}, u32[]{:S(2)}) collective-permute-start(bf16[2048,256]{1,0:T(8,128)(2,1)} %refs_0_.3), channel_id=1, source_target_pairs={{0,4},{4,0},{1,5},{5,1},{2,6},{6,2},{3,7},{7,3},{8,12},{12,8},{9,1... | collective-permute-start | bytes 3145736 | tf_op jit(solution)/shard_map/ppermute | solution.py:166
  22.6 9.1 %copy-start = (bf16[1024,1024]{1,0:T(8,128)(2,1)S(1)}, bf16[1024,1024]{1,0:T(8,128)(2,1)}, u32[]{:S(2)}) copy-start(bf16[1024,1024]{1,0:T(8,128)(2,1)} %shard_map.163) | copy-start | bytes 6291460
  25.2 84.3 %collective-permute-start.1 = (bf16[1024,1024]{1,0:T(8,128)(2,1)}, bf16[1024,1024]{1,0:T(8,128)(2,1)}, u32[]{:S(2)}, u32[]{:S(2)}) collective-permute-start(bf16[1024,1024]{1,0:T(8,128)(2,1)} %shard_map.163), channel_id=1, source_target_pairs={{0,4},{4,0},{1,5},{5,1},{2,6},{6,2},{3,7},{7,3},{8,12},{12,8},{9,1... | collective-permute-start | bytes 6291464 | tf_op jit(solution)/shard_map/ppermute | solution.py:166
  27.2 104.8 %collective-permute-start.2 = (bf16[512,1024]{1,0:T(8,128)(2,1)}, bf16[512,1024]{1,0:T(8,128)(2,1)}, u32[]{:S(2)}, u32[]{:S(2)}) collective-permute-start(bf16[512,1024]{1,0:T(8,128)(2,1)} %shard_map.164), channel_id=1, source_target_pairs={{0,4},{4,0},{1,5},{5,1},{2,6},{6,2},{3,7},{7,3},{8,12},{12,8},{9,1... | collective-permute-start | bytes 3145736 | tf_op jit(solution)/shard_map/ppermute | solution.py:166
  33.2 6.1 %copy-start.1 = (bf16[512,1024]{1,0:T(8,128)(2,1)S(1)}, bf16[512,1024]{1,0:T(8,128)(2,1)}, u32[]{:S(2)}) copy-start(bf16[512,1024]{1,0:T(8,128)(2,1)} %shard_map.164) | copy-start | bytes 3145732
  35.2 7.0 %copy-start.4 = (bf16[128,1024]{1,0:T(8,128)(2,1)S(1)}, bf16[128,1024]{1,0:T(8,128)(2,1)}, u32[]{:S(2)}) copy-start(bf16[128,1024]{1,0:T(8,128)(2,1)} %shard_map.166) | copy-start | bytes 786436
  37.1 5.9 %copy-start.3 = (bf16[128,1024]{1,0:T(8,128)(2,1)S(1)}, bf16[128,1024]{1,0:T(8,128)(2,1)}, u32[]{:S(2)}) copy-start(bf16[128,1024]{1,0:T(8,128)(2,1)} %shard_map.167) | copy-start | bytes 786436
  43.7 99.4 %collective-permute-start.3 = (bf16[256,1024]{1,0:T(8,128)(2,1)}, bf16[256,1024]{1,0:T(8,128)(2,1)S(1)}, u32[]{:S(2)}, u32[]{:S(2)}) collective-permute-start(bf16[256,1024]{1,0:T(8,128)(2,1)} %shard_map.165), channel_id=1, source_target_pairs={{0,4},{4,0},{1,5},{5,1},{2,6},{6,2},{3,7},{7,3},{8,12},{12,8},{9,1... | collective-permute-start | bytes 1572872 | tf_op jit(solution)/shard_map/ppermute | solution.py:166
  59.2 1.1 copy-start.2
  59.2 89.5 %collective-permute-start.4 = (bf16[128,1024]{1,0:T(8,128)(2,1)S(1)}, bf16[128,1024]{1,0:T(8,128)(2,1)S(1)}, u32[]{:S(2)}, u32[]{:S(2)}) collective-permute-start(bf16[128,1024]{1,0:T(8,128)(2,1)S(1)} %copy-done.4), channel_id=1, source_target_pairs={{0,4},{4,0},{1,5},{5,1},{2,6},{6,2},{3,7},{7,3},{8,12},{12,8},{9,1... | collective-permute-start | bytes 786440 | tf_op jit(solution)/shard_map/ppermute | solution.py:166
  66.7 86.2 %collective-permute-start.5 = (bf16[128,1024]{1,0:T(8,128)(2,1)S(1)}, bf16[128,1024]{1,0:T(8,128)(2,1)S(1)}, u32[]{:S(2)}, u32[]{:S(2)}) collective-permute-start(bf16[128,1024]{1,0:T(8,128)(2,1)S(1)} %copy-done.3), channel_id=1, source_target_pairs={{0,4},{4,0},{1,5},{5,1},{2,6},{6,2},{3,7},{7,3},{8,12},{12,8},{9,1... | collective-permute-start | bytes 786440 | tf_op jit(solution)/shard_map/ppermute | solution.py:166
where the time goes:
time: 154 us
  waiting for transfers between devices  72 us (47%)
  Pallas kernels  32.5 us (21%)
  local copies, waits for them, and re-layouts  26.5 us (17%)
  starting transfers between devices  10.6 us (7%)
  blocking collectives  10 us (6%)
    ppermute x9, waiting for transfers between devices, shifted(): lax.ppermute(array, 'zero', [(i, (i + k) % n) for i in range(n)])  72 us
    pallas_call x6, Pallas kernels, own_rows(): pl.pallas_call(kernel, grid=(size // tile,), out_shape=out_shape, in_spec...  19.7 us
    pallas_call x2, Pallas kernels, finish(): pl.pallas_call(functools.partial(finish_kernel, n, rows, tile, extra), gr...  12.8 us
    ppermute x9, starting transfers between devices, shifted(): lax.ppermute(array, 'zero', [(i, (i + k) % n) for i in range(n)])  10.6 us
    all_gather x1, blocking collectives, on_device(): packs = lax.all_gather(packs, 'tp', axis=2, tiled=True)  10 us
    dynamic_update_slice x5, local copies, waits for them, and re-layouts, on_device(): lax.dynamic_update_slice(serve_query, chunk, (owner * rows + start, 0))  7.61 us
    dynamic_update_slice x5, local copies, waits for them, and re-layouts, on_device(): lax.dynamic_update_slice(serve_query, chunk, (me * rows + start, 0))  5.83 us
    broadcast_in_dim x1, local copies, waits for them, and re-layouts, on_device(): serve_query = jnp.zeros((n * rows, weight_query.shape[1]), jnp.bfloat16)  4.47 us
  transfers between devices with their start and end apart: 9, of which 5 were waited for; matrix products, arithmetic and copies ran while one was open for 16% of the time, Pallas kernels for 17%

commit v1 on v0

--- a/solution.py
+++ b/solution.py
@@ -142,6 +142,27 @@
     )(*args)
 
 
+def store_kernel(n, shift, rows, start, chunk_ref, _, out_ref, sem):
+    owner = lax.rem(lax.axis_index("zero") + n - shift, n)
+    at = pl.ds(pl.multiple_of(owner * rows + start, chunk_ref.shape[0]), chunk_ref.shape[0])
+    copy = pltpu.make_async_copy(chunk_ref, out_ref.at[at], sem)
+    copy.start()
+    copy.wait()
+
+
+def store_rows(n, shift, rows, start, chunk, whole):
+    return pl.pallas_call(
+        functools.partial(store_kernel, n, shift, rows, start),
+        out_shape=jax.ShapeDtypeStruct(whole.shape, whole.dtype),
+        in_specs=[pl.BlockSpec(memory_space=pltpu.VMEM), pl.BlockSpec(memory_space=pl.ANY)],
+        out_specs=pl.BlockSpec(memory_space=pl.ANY),
+        scratch_shapes=[pltpu.SemaphoreType.DMA],
+        input_output_aliases={1: 0},
+        compiler_params=pltpu.CompilerParams(vmem_limit_bytes=8 * 2**20),
+        cost_estimate=pl.CostEstimate(flops=0, bytes_accessed=4 * chunk.size, transcendentals=0),
+    )(chunk, whole)
+
+
 def on_device(
     n,
     parts,
@@ -222,6 +243,9 @@
         serve_query = lax.dynamic_update_slice(serve_query, chunk, (me * rows + start, 0))
     for start, arrived in theirs:
         for k, chunk in enumerate(arrived):
+            if start + chunk.shape[0] == rows:
+                serve_query = store_rows(n, k + 1, rows, start, chunk, serve_query)
+                continue
             owner = (me + n - 1 - k) % n
             serve_query = lax.dynamic_update_slice(serve_query, chunk, (owner * rows + start, 0))
     return (

time: 154 us -> 155 us (level)
    dynamic_update_slice x5 -> x4, local copies, waits for them, and re-layouts: 7.61 us -> 6.89 us  [on_device(): lax.dynamic_update_slice(serve_query, chunk, (owner * rows + start, 0))]
  transfers between devices with their start and end apart: 9 -> 9, of which waited for: 5 -> 5; matrix products, arithmetic and copies ran while one was open for 16% -> 17% of each run, Pallas kernels for 17% -> 17%
where the time goes in v1:
time: 155 us; the launch traced here: 154 us
  waiting for transfers between devices  71.3 us (46%)
  Pallas kernels  33.2 us (21%)
  local copies, waits for them, and re-layouts  27.3 us (18%)
  starting transfers between devices  10.5 us (7%)
  blocking collectives  10 us (6%)
    ppermute x9, waiting for transfers between devices, shifted(): lax.ppermute(array, 'zero', [(i, (i + k) % n) for i in range(n)])  71.3 us
    pallas_call x6, Pallas kernels, own_rows(): pl.pallas_call(kernel, grid=(size // tile,), out_shape=out_shape, in_spec...  19.7 us
    pallas_call x2, Pallas kernels, finish(): pl.pallas_call(functools.partial(finish_kernel, n, rows, tile, extra), gr...  12.8 us
    ppermute x9, starting transfers between devices, shifted(): lax.ppermute(array, 'zero', [(i, (i + k) % n) for i in range(n)])  10.5 us
    all_gather x1, blocking collectives, on_device(): packs = lax.all_gather(packs, 'tp', axis=2, tiled=True)  10 us
    dynamic_update_slice x4, local copies, waits for them, and re-layouts, on_device(): lax.dynamic_update_slice(serve_query, chunk, (owner * rows + start, 0))  6.89 us
    dynamic_update_slice x5, local copies, waits for them, and re-layouts, on_device(): lax.dynamic_update_slice(serve_query, chunk, (me * rows + start, 0))  5.83 us
    broadcast_in_dim x1, local copies, waits for them, and re-layouts, on_device(): serve_query = jnp.zeros((n * rows, weight_query.shape[1]), jnp.bfloat16)  4.47 us
  transfers between devices with their start and end apart: 9, of which 5 were waited for; matrix products, arithmetic and copies ran while one was open for 17% of the time, Pallas kernels for 17%

profile of v1, /device:TPU:0, one launch (start us, length us, event | category | flops | bytes accessed | tf_op | source)
XLA Modules:
  0.0 154.4 jit_solution(7538862599674937791)
XLA Ops:
  0.6 1.9 %copy.28.low_ref = bf16[2048,32]{1,0:T(8,128)(2,1)} copy(bf16[2048,32]{0,1:T(8,128)(2,1)} %param.12) | data formatting | bytes 262144 | tf_op args[1]
  2.5 6.7 %shard_map.162 = f32[1,1024]{1,0:T(1,128)} custom-call(bf16[2048,1024]{1,0:T(8,128)(2,1)} %weight_ref.11, bf16[2048,32]{1,0:T(8,128)(2,1)} %copy.28.low_ref, bf16[32,1024]{1,0:T(8,128)(2,1)} %high_ref.11), custom_call_target="tpu_custom_call" | custom-call | flops 134217728 | bytes 8388608 | tf_op jit(solution)/shard_map/pallas_call | solution.py:133
  9.2 3.0 %collective-permute-start = (f32[1,1024]{1,0:T(1,128)}, f32[1,1024]{1,0:T(1,128)S(1)}, u32[]{:S(2)}, u32[]{:S(2)}) collective-permute-start(f32[1,1024]{1,0:T(1,128)} %shard_map.162), channel_id=1, source_target_pairs={{0,4},{4,0},{1,5},{5,1},{2,6},{6,2},{3,7},{7,3},{8,12},{12,8},{9,1... | collective-permute-start | bytes 12296 | tf_op jit(solution)/shard_map/ppermute | solution.py:187
  12.2 0.8 constant_dynamic-slice_fusion
  13.0 0.1 copy.38
  13.1 0.1 copy.39
  13.2 0.7 add_convert_fusion
  13.9 0.1 reshape.46
  14.1 0.1 pad_maximum_fusion.1
  14.2 0.1 copy.36
  14.3 0.7 reshape.42
  15.0 0.0 collective-permute-start.7
  15.0 2.0 %collective-permute-start.8 = (bf16[2048,256]{1,0:T(8,128)(2,1)}, bf16[2048,256]{1,0:T(8,128)(2,1)S(1)}, u32[]{:S(2)}, u32[]{:S(2)}) collective-permute-start(bf16[2048,256]{1,0:T(8,128)(2,1)} %refs_0_.2), channel_id=1, source_target_pairs={{0,4},{4,0},{1,5},{5,1},{2,6},{6,2},{3,7},{7,3},{8,12},{12,8},{9,1... | collective-permute-start | bytes 3145736 | tf_op jit(solution)/shard_map/ppermute | solution.py:187
  17.1 0.0 collective-permute-start.6
  17.1 0.1 fusion.1
  17.3 0.7 dynamic_update_slice.39
  18.1 0.0 collective-permute-done
  18.1 0.1 dynamic_update_slice.40
  18.1 0.6 sqrt.5
  18.7 4.3 %shard_map.164 = bf16[1024,1024]{1,0:T(8,128)(2,1)} custom-call(bf16[2048,1024]{1,0:T(8,128)(2,1)} %weight_ref.11, bf16[2048,32]{1,0:T(8,128)(2,1)} %copy.28.low_ref, bf16[32,1024]{1,0:T(8,128)(2,1)} %high_ref.11, f32[1,1024]{1,0:T(1,128)} %bitcast.15), custom_call_target="tpu_custom_call" | custom-call | flops 67108864 | bytes 4194304 | tf_op jit(solution)/shard_map/pallas_call | solution.py:133
  23.1 2.6 %shard_map.165 = bf16[512,1024]{1,0:T(8,128)(2,1)} custom-call(bf16[2048,1024]{1,0:T(8,128)(2,1)} %weight_ref.11, bf16[2048,32]{1,0:T(8,128)(2,1)} %copy.28.low_ref, bf16[32,1024]{1,0:T(8,128)(2,1)} %high_ref.11, f32[1,1024]{1,0:T(1,128)} %bitcast.16), custom_call_target="tpu_custom_call" | custom-call | flops 33554432 | bytes 2097152 | tf_op jit(solution)/shard_map/pallas_call | solution.py:133
  25.7 2.0 %collective-permute-start.2 = (bf16[1024,1024]{1,0:T(8,128)(2,1)}, bf16[1024,1024]{1,0:T(8,128)(2,1)}, u32[]{:S(2)}, u32[]{:S(2)}) collective-permute-start(bf16[1024,1024]{1,0:T(8,128)(2,1)} %shard_map.164), channel_id=1, source_target_pairs={{0,4},{4,0},{1,5},{5,1},{2,6},{6,2},{3,7},{7,3},{8,12},{12,8},{9,1... | collective-permute-start | bytes 6291464 | tf_op jit(solution)/shard_map/ppermute | solution.py:187
  27.7 0.0 collective-permute-start.3
  27.7 4.5 %broadcast_in_dim.11 = bf16[4096,1024]{1,0:T(8,128)(2,1)} broadcast(bf16[]{:T(256)} %constant.60.clone.1), dimensions={} | broadcast | bytes 8388610 | tf_op jit(solution)/shard_map/broadcast_in_dim | solution.py:241
  32.2 0.0 copy-done
  32.2 1.5 constant_dynamic-update-slice_fusion.8
  33.7 2.0 %shard_map.167 = bf16[128,1024]{1,0:T(8,128)(2,1)} custom-call(bf16[2048,1024]{1,0:T(8,128)(2,1)} %weight_ref.11, bf16[2048,32]{1,0:T(8,128)(2,1)} %copy.28.low_ref, bf16[32,1024]{1,0:T(8,128)(2,1)} %high_ref.11, f32[1,1024]{1,0:T(1,128)} %bitcast.17), custom_call_target="tpu_custom_call" | custom-call | flops 8388608 | bytes 524288 | tf_op jit(solution)/shard_map/pallas_call | solution.py:133
  35.6 1.9 %shard_map.163 = bf16[128,1024]{1,0:T(8,128)(2,1)} custom-call(bf16[2048,1024]{1,0:T(8,128)(2,1)} %weight_ref.11, bf16[2048,32]{1,0:T(8,128)(2,1)} %copy.28.low_ref, bf16[32,1024]{1,0:T(8,128)(2,1)} %high_ref.11, f32[1,1024]{1,0:T(1,128)} %bitcast.18), custom_call_target="tpu_custom_call" | custom-call | flops 8388608 | bytes 524288 | tf_op jit(solution)/shard_map/pallas_call | solution.py:133
  37.6 2.2 %shard_map.166 = bf16[256,1024]{1,0:T(8,128)(2,1)} custom-call(bf16[2048,1024]{1,0:T(8,128)(2,1)} %weight_ref.11, bf16[2048,32]{1,0:T(8,128)(2,1)} %copy.28.low_ref, bf16[32,1024]{1,0:T(8,128)(2,1)} %high_ref.11, f32[1,1024]{1,0:T(1,128)} %bitcast.19), custom_call_target="tpu_custom_call" | custom-call | flops 16777216 | bytes 1048576 | tf_op jit(solution)/shard_map/pallas_call | solution.py:133
  39.8 0.0 copy-done.1
  39.8 1.0 constant_dynamic-update-slice_fusion.7
  40.8 1.9 %constant_dynamic-update-slice_fusion.6 = bf16[4096,1024]{1,0:T(8,128)(2,1)} fusion(bf16[4096,1024]{1,0:T(8,128)(2,1)} %constant_dynamic-update-slice_fusion.7, bf16[256,1024]{1,0:T(8,128)(2,1)} %shard_map.166, s32[]{:T(128)S(6)} %select_n.68), kind=kLoop, calls=%fused_computation.13 | loop fusion | bytes 1048580 | tf_op jit(solution)/shard_map/dynamic_update_slice | solution.py:243
  42.7 0.0 copy-done.4
  42.7 0.7 constant_dynamic-update-slice_fusion.5
  43.4 0.7 constant_dynamic-update-slice_fusion.4
  44.2 0.0 collective-permute-done.7
  44.2 2.0 %collective-permute-start.4 = (bf16[256,1024]{1,0:T(8,128)(2,1)}, bf16[256,1024]{1,0:T(8,128)(2,1)S(1)}, u32[]{:S(2)}, u32[]{:S(2)}) collective-permute-start(bf16[256,1024]{1,0:T(8,128)(2,1)} %shard_map.166), channel_id=1, source_target_pairs={{0,4},{4,0},{1,5},{5,1},{2,6},{6,2},{3,7},{7,3},{8,12},{12,8},{9,1... | collective-permute-start | bytes 1572872 | tf_op jit(solution)/shard_map/ppermute | solution.py:187
  46.1 0.9 stack_reshape.3
  47.1 0.1 copy.37
  47.2 0.1 pad_maximum_fusion
  47.3 10.0 %all_gather.3 = bf16[2,65,2048]{1,2,0:T(8,128)(2,1)S(1)} all-gather(bf16[2,65,512]{1,2,0:T(8,128)(2,1)S(1)} %pad_maximum_fusion), channel_id=1, replica_groups=mesh['unit'=4,'zero'=2,'tp'=4] {'tp'}, dimensions={2}, use_global_device_ids=true | all-gather | bytes 665600 | tf_op jit(solution)/shard_map/all_gather | solution.py:230
  57.3 0.1 slice_bitcast_fusion
  57.4 1.7 %fusion = (bf16[2,2048,32]{2,1,0:T(8,128)(2,1)}, bf16[2,2048,32]{2,1,0:T(8,128)(2,1)}) fusion(bf16[2,2048,64]{2,1,0:T(8,128)(2,1)S(1)} %slice_bitcast_fusion), kind=kLoop, calls=%fused_computation.17 | loop fusion | bytes 1048576 | tf_op jit(solution)/shard_map/slice | solution.py:236
  59.1 0.7 slice_reduce_fusion
  59.9 0.1 dynamic_update_slice.50
  59.9 0.1 dynamic_update_slice.51
  60.0 0.6 copy.40
  60.6 0.0 collective-permute-done.8.refs_1_
  60.6 0.5 collective-permute-start.5
  61.2 0.5 copy-done.2
  61.7 6.4 %shard_map.169 = (bf16[4096,256]{1,0:T(8,128)(2,1)}, f32[1,256]{1,0:T(1,128)}) custom-call(bf16[2048,256]{1,0:T(8,128)(2,1)} %refs_0_.2, bf16[2048,256]{1,0:T(8,128)(2,1)} %copy-done.2, bf16[2,2048,32]{2,1,0:T(8,128)(2,1)} %get-tuple-element.17.refs_2_, bf16[32,256]{1,0:T(8,128)(2,1)} %refs_3_.2), custom_call_target="tpu_custom_call" | custom-call | flops 67108864 | bytes 8388608 | tf_op jit(solution)/shard_map/pallas_call | solution.py:66
  68.1 0.0 collective-permute-done.6.refs_1_
  68.1 1.0 collective-permute-start.1
  69.1 6.4 %shard_map.170 = (bf16[4096,256]{1,0:T(8,128)(2,1)}, f32[1,256]{1,0:T(1,128)}) custom-call(bf16[2048,256]{1,0:T(8,128)(2,1)} %refs_0_.3, bf16[2048,256]{1,0:T(8,128)(2,1)} %collective-permute-done.6.refs_1_, bf16[2,2048,32]{2,1,0:T(8,128)(2,1)} %get-tuple-element.18.refs_2_, bf16[32,256]{1,0:T(8,128)(2,1)} %refs_3_.3, f32[1,256]{1,0:T(1,128)} %get-tuple-element.11.refs_4_), custom_call_target="tpu_custom_call" | custom-call | flops 67108864 | bytes 8388608 | tf_op jit(solution)/shard_map/pallas_call | solution.py:66
  75.5 34.8 %collective-permute-done.2 = bf16[1024,1024]{1,0:T(8,128)(2,1)} collective-permute-done((bf16[1024,1024]{1,0:T(8,128)(2,1)}, bf16[1024,1024]{1,0:T(8,128)(2,1)}, u32[]{:S(2)}, u32[]{:S(2)}) %collective-permute-start.2) | collective-permute-done | bytes 2097184 | tf_op jit(solution)/shard_map/ppermute | solution.py:187
  110.2 3.1 %constant_dynamic-update-slice_fusion.3 = bf16[4096,1024]{1,0:T(8,128)(2,1)} fusion(bf16[4096,1024]{1,0:T(8,128)(2,1)} %constant_dynamic-update-slice_fusion.4, bf16[1024,1024]{1,0:T(8,128)(2,1)} %collective-permute-done.2, s32[]{:T(128)S(6)} %select_n.71), kind=kLoop, calls=%fused_computation.10 | loop fusion | bytes 4194308 | tf_op jit(solution)/shard_map/dynamic_update_slice | solution.py:250
  113.3 19.4 %collective-permute-done.3 = bf16[512,1024]{1,0:T(8,128)(2,1)} collective-permute-done((bf16[512,1024]{1,0:T(8,128)(2,1)}, bf16[512,1024]{1,0:T(8,128)(2,1)}, u32[]{:S(2)}, u32[]{:S(2)}) %collective-permute-start.3) | collective-permute-done | bytes 1048608 | tf_op jit(solution)/shard_map/ppermute | solution.py:187
  132.7 2.3 %constant_dynamic-update-slice_fusion.2 = bf16[4096,1024]{1,0:T(8,128)(2,1)} fusion(bf16[4096,1024]{1,0:T(8,128)(2,1)} %constant_dynamic-update-slice_fusion.3, bf16[512,1024]{1,0:T(8,128)(2,1)} %collective-permute-done.3, s32[]{:T(128)S(6)} %select_n.72), kind=kLoop, calls=%fused_computation.9 | loop fusion | bytes 2097156 | tf_op jit(solution)/shard_map/dynamic_update_slice | solution.py:250
  135.0 8.9 %collective-permute-done.4 = bf16[256,1024]{1,0:T(8,128)(2,1)S(1)} collective-permute-done((bf16[256,1024]{1,0:T(8,128)(2,1)}, bf16[256,1024]{1,0:T(8,128)(2,1)S(1)}, u32[]{:S(2)}, u32[]{:S(2)}) %collective-permute-start.4) | collective-permute-done | bytes 524320 | tf_op jit(solution)/shard_map/ppermute | solution.py:187
  143.8 0.8 constant_dynamic-update-slice_fusion.1
  144.7 4.8 %collective-permute-done.5 = bf16[128,1024]{1,0:T(8,128)(2,1)S(1)} collective-permute-done((bf16[128,1024]{1,0:T(8,128)(2,1)S(1)}, bf16[128,1024]{1,0:T(8,128)(2,1)S(1)}, u32[]{:S(2)}, u32[]{:S(2)}) %collective-permute-start.5) | collective-permute-done | bytes 262176 | tf_op jit(solution)/shard_map/ppermute | solution.py:187
  149.5 0.7 constant_dynamic-update-slice_fusion._
  150.2 3.5 %collective-permute-done.1.chunk_ref = bf16[128,1024]{1,0:T(8,128)(2,1)S(1)} collective-permute-done((bf16[128,1024]{1,0:T(8,128)(2,1)S(1)}, bf16[128,1024]{1,0:T(8,128)(2,1)S(1)}, u32[]{:S(2)}, u32[]{:S(2)}) %collective-permute-start.1) | collective-permute-done | bytes 262176 | tf_op jit(solution)/shard_map/ppermute | solution.py:187
  153.7 0.7 shard_map.168
  (11 shorter events, 0.1 us)
Async XLA Ops:
  9.2 8.8 %collective-permute-start = (f32[1,1024]{1,0:T(1,128)}, f32[1,1024]{1,0:T(1,128)S(1)}, u32[]{:S(2)}, u32[]{:S(2)}) collective-permute-start(f32[1,1024]{1,0:T(1,128)} %shard_map.162), channel_id=1, source_target_pairs={{0,4},{4,0},{1,5},{5,1},{2,6},{6,2},{3,7},{7,3},{8,12},{12,8},{9,1... | collective-permute-start | bytes 12296 | tf_op jit(solution)/shard_map/ppermute | solution.py:187
  15.0 29.1 %collective-permute-start.7 = (bf16[260,128]{1,0:T(8,128)(2,1)}, bf16[260,128]{1,0:T(8,128)(2,1)}, u32[]{:S(2)}, u32[]{:S(2)}) collective-permute-start(bf16[260,128]{1,0:T(8,128)(2,1)} %reshape.42), channel_id=1, source_target_pairs={{0,4},{4,0},{1,5},{5,1},{2,6},{6,2},{3,7},{7,3},{8,12},{12,8},{9,1... | collective-permute-start | bytes 199688 | tf_op jit(solution)/shard_map/ppermute | solution.py:187
  15.0 45.6 %collective-permute-start.8 = (bf16[2048,256]{1,0:T(8,128)(2,1)}, bf16[2048,256]{1,0:T(8,128)(2,1)S(1)}, u32[]{:S(2)}, u32[]{:S(2)}) collective-permute-start(bf16[2048,256]{1,0:T(8,128)(2,1)} %refs_0_.2), channel_id=1, source_target_pairs={{0,4},{4,0},{1,5},{5,1},{2,6},{6,2},{3,7},{7,3},{8,12},{12,8},{9,1... | collective-permute-start | bytes 3145736 | tf_op jit(solution)/shard_map/ppermute | solution.py:187
  17.1 51.1 %collective-permute-start.6 = (bf16[2048,256]{1,0:T(8,128)(2,1)}, bf16[2048,256]{1,0:T(8,128)(2,1)}, u32[]{:S(2)}, u32[]{:S(2)}) collective-permute-start(bf16[2048,256]{1,0:T(8,128)(2,1)} %refs_0_.3), channel_id=1, source_target_pairs={{0,4},{4,0},{1,5},{5,1},{2,6},{6,2},{3,7},{7,3},{8,12},{12,8},{9,1... | collective-permute-start | bytes 3145736 | tf_op jit(solution)/shard_map/ppermute | solution.py:187
  23.1 9.1 %copy-start = (bf16[1024,1024]{1,0:T(8,128)(2,1)S(1)}, bf16[1024,1024]{1,0:T(8,128)(2,1)}, u32[]{:S(2)}) copy-start(bf16[1024,1024]{1,0:T(8,128)(2,1)} %shard_map.164) | copy-start | bytes 6291460
  25.7 84.5 %collective-permute-start.2 = (bf16[1024,1024]{1,0:T(8,128)(2,1)}, bf16[1024,1024]{1,0:T(8,128)(2,1)}, u32[]{:S(2)}, u32[]{:S(2)}) collective-permute-start(bf16[1024,1024]{1,0:T(8,128)(2,1)} %shard_map.164), channel_id=1, source_target_pairs={{0,4},{4,0},{1,5},{5,1},{2,6},{6,2},{3,7},{7,3},{8,12},{12,8},{9,1... | collective-permute-start | bytes 6291464 | tf_op jit(solution)/shard_map/ppermute | solution.py:187
  27.7 105.0 %collective-permute-start.3 = (bf16[512,1024]{1,0:T(8,128)(2,1)}, bf16[512,1024]{1,0:T(8,128)(2,1)}, u32[]{:S(2)}, u32[]{:S(2)}) collective-permute-start(bf16[512,1024]{1,0:T(8,128)(2,1)} %shard_map.165), channel_id=1, source_target_pairs={{0,4},{4,0},{1,5},{5,1},{2,6},{6,2},{3,7},{7,3},{8,12},{12,8},{9,1... | collective-permute-start | bytes 3145736 | tf_op jit(solution)/shard_map/ppermute | solution.py:187
  33.7 6.1 %copy-start.1 = (bf16[512,1024]{1,0:T(8,128)(2,1)S(1)}, bf16[512,1024]{1,0:T(8,128)(2,1)}, u32[]{:S(2)}) copy-start(bf16[512,1024]{1,0:T(8,128)(2,1)} %shard_map.165) | copy-start | bytes 3145732
  35.6 7.1 %copy-start.4 = (bf16[128,1024]{1,0:T(8,128)(2,1)S(1)}, bf16[128,1024]{1,0:T(8,128)(2,1)}, u32[]{:S(2)}) copy-start(bf16[128,1024]{1,0:T(8,128)(2,1)} %shard_map.167) | copy-start | bytes 786436
  37.6 5.9 %copy-start.3 = (bf16[128,1024]{1,0:T(8,128)(2,1)S(1)}, bf16[128,1024]{1,0:T(8,128)(2,1)}, u32[]{:S(2)}) copy-start(bf16[128,1024]{1,0:T(8,128)(2,1)} %shard_map.163) | copy-start | bytes 786436
  44.2 99.7 %collective-permute-start.4 = (bf16[256,1024]{1,0:T(8,128)(2,1)}, bf16[256,1024]{1,0:T(8,128)(2,1)S(1)}, u32[]{:S(2)}, u32[]{:S(2)}) collective-permute-start(bf16[256,1024]{1,0:T(8,128)(2,1)} %shard_map.166), channel_id=1, source_target_pairs={{0,4},{4,0},{1,5},{5,1},{2,6},{6,2},{3,7},{7,3},{8,12},{12,8},{9,1... | collective-permute-start | bytes 1572872 | tf_op jit(solution)/shard_map/ppermute | solution.py:187
  60.6 1.1 copy-start.2
  60.6 88.8 %collective-permute-start.5 = (bf16[128,1024]{1,0:T(8,128)(2,1)S(1)}, bf16[128,1024]{1,0:T(8,128)(2,1)S(1)}, u32[]{:S(2)}, u32[]{:S(2)}) collective-permute-start(bf16[128,1024]{1,0:T(8,128)(2,1)S(1)} %copy-done.4), channel_id=1, source_target_pairs={{0,4},{4,0},{1,5},{5,1},{2,6},{6,2},{3,7},{7,3},{8,12},{12,8},{9,1... | collective-permute-start | bytes 786440 | tf_op jit(solution)/shard_map/ppermute | solution.py:187
  68.1 85.5 %collective-permute-start.1 = (bf16[128,1024]{1,0:T(8,128)(2,1)S(1)}, bf16[128,1024]{1,0:T(8,128)(2,1)S(1)}, u32[]{:S(2)}, u32[]{:S(2)}) collective-permute-start(bf16[128,1024]{1,0:T(8,128)(2,1)S(1)} %copy-done.3), channel_id=1, source_target_pairs={{0,4},{4,0},{1,5},{5,1},{2,6},{6,2},{3,7},{7,3},{8,12},{12,8},{9,1... | collective-permute-start | bytes 786440 | tf_op jit(solution)/shard_map/ppermute | solution.py:187
